TPU v7x, 512 devices: a whole 4x8x8 slice. The times are simulated.
512 devices in a mesh: pb: 8 (over x, core), ka: 64 (over z, y).
Axes of the slice: x: 4, y: 8, z: 8, core: 2. Of those that a mesh axis runs over, the one named last changes fastest.
Arguments:
- coupling: bfloat16 [8, 64, 128, 32, 384], P('pb', 'ka'), may hold values from -0.796875 to 0.796875
- phonon_occ: float32 [8, 64, 128, 12], P('pb', 'ka'), may hold values from 0.1 to 1
- band_window: int32 [8, 64, 128, 32], P('pb', 'ka'), may hold values 0 or 1
- pair_count: int32 [8, 64, 64], P('pb', 'ka'), may hold values from 0 to 2, as said below
- k_target: int32 [8, 64, 128], P('pb', 'ka'), may hold values from 0 to 127
- kq_source: int32 [8, 64, 128], P('pb', 'ka'), may hold values from 0 to 127
- velocity: float32 [3, 32, 8192], P(None, None, 'ka'), may hold values from -6 to 6
- lifetime: float32 [32, 8192], P(None, 'ka'), may hold values from 0.5 to 2
Outputs:
- deviation: float32 [3, 32, 8192], P(None, None, 'ka')
Inputs may be any that keep to these rules, and one draw needn't show every extreme that they name: pair_count[p, a, d] is the number of live tile slots among slots d * 2 to d * 2 + 1 of device (p, a); in every q-group p some owner d receives 2 live tiles from every source.
All inputs are finite; a program needn't handle non-finite values. No bound on the sum of `band_window` on one device may be relied on, other than what follows from the above.
Results may differ from a plain program's by a relative error of at most 0.012.
Values may be sent and summed in bfloat16 or wider, within the bound.
No kernel may reach another device: no remote copies, remote signals or barrier semaphores. Data moves between devices by JAX's collectives and lax.ppermute only.
A program may use at most 64 MiB of HBM per device.

v0:
```python
import jax
import jax.numpy as jnp
from jax import lax
from jax.sharding import PartitionSpec as P

MODES = 12
TILE_SLOTS = 2
ITERS = 4


def from_everyone(x, axis):
    copies = jnp.broadcast_to(x, (lax.axis_size(axis), *x.shape))
    return lax.all_to_all(copies, axis, split_axis=0, concat_axis=0, tiled=True)


def of_everyone(x, axis):
    return from_everyone(x, axis).astype(jnp.float32).sum(axis=0)


def tile_terms(weight, chosen):
    return jnp.einsum("tnm,dmt->dnt", weight, chosen, preferred_element_type=jnp.float32)


def shards(coupling, phonon_occ, band_window, pair_count, k_target, kq_source, velocity, lifetime):
    tile_count = coupling.shape[2]
    block_width = velocity.shape[2]
    directions = velocity.shape[0]
    band_count = velocity.shape[1]
    slot_live = (
        (jnp.arange(TILE_SLOTS)[None, :] < pair_count[0, 0][:, None])
        .reshape(tile_count)
        .astype(jnp.float32)
    )
    window = band_window[0, 0].astype(jnp.float32) * slot_live[:, None]
    widened = coupling[0, 0].astype(jnp.float32)
    squared = (widened * widened).reshape(tile_count, band_count, band_count, MODES)
    summed = jnp.sum(squared * phonon_occ[0, 0][:, None, None, :], axis=3)
    weight = (summed * window[:, :, None]).astype(jnp.bfloat16)
    targets = lax.all_to_all(k_target[0, 0], "ka", split_axis=0, concat_axis=0, tiled=True)
    onehot = (targets[:, None] == jnp.arange(block_width, dtype=jnp.int32)[None, :]).astype(
        jnp.float32
    )
    deviation = lifetime[None] * velocity
    for iteration in range(ITERS):
        rounded = deviation.astype(jnp.bfloat16)
        local_terms = tile_terms(weight, jnp.take(rounded, kq_source[0, 0], axis=2))
        contribution = lax.all_to_all(
            local_terms.astype(jnp.bfloat16), "ka", split_axis=2, concat_axis=2, tiled=True
        ).astype(local_terms.dtype)
        partial_value = jnp.dot(
            contribution.reshape(directions * band_count, tile_count),
            onehot,
            precision=lax.Precision.HIGHEST,
            preferred_element_type=jnp.float32,
        )
        partial_value = partial_value.reshape(directions, band_count, block_width)
        scattering = of_everyone(partial_value.astype(jnp.bfloat16), "pb").astype(jnp.float32)
        deviation = lifetime[None] * (velocity + scattering)
    return deviation


def solution(mesh):
    placed = (
        P("pb", "ka", None, None, None),
        P("pb", "ka", None, None),
        P("pb", "ka", None, None),
        P("pb", "ka", None),
        P("pb", "ka", None),
        P("pb", "ka", None),
        P(None, None, "ka"),
        P(None, "ka"),
    )
    return jax.shard_map(
        shards, mesh=mesh, in_specs=placed, out_specs=P(None, None, "ka"), check_vma=False
    )
```

profile of v0, /device:TPU:1, one launch (start us, length us, event | category | flops | bytes accessed | tf_op | source)
XLA Modules:
  0.0 157.2 jit_solution(8152493061816729378)
XLA Ops:
  0.0 0.5 broadcast.93
  0.5 1.2 reduce.6
  1.8 0.8 all_to_all.31
  2.5 17.1 %all-to-all-start.1 = ((s32[64,2,1]{1,2,0:T(1,128)}), s32[64,2,1]{1,2,0:T(1,128)S(1)}, u32[]{:S(2)}, u32[]{:S(2)}) async-start(s32[64,2,1]{1,2,0:T(1,128)} %bitcast.6), calls=%async_computation.1 | async-start | bytes 65536 | tf_op jit(solution)/shard_map/all_to_all | solution.py:39
  19.7 0.7 compare_select_fusion
  20.3 0.7 compare_and_fusion
  21.0 0.0 copy-start.3
  21.0 4.6 %copy.62 = bf16[1,1,128,32,384]{2,3,4,1,0:T(8,128)(2,1)S(1)} copy(bf16[1,1,128,32,384]{4,3,2,1,0:T(8,128)(2,1)} %param.10) | data formatting | bytes 6291456 | tf_op args[0]
  25.6 0.0 copy-start.4
  25.6 0.0 copy-start.2
  25.6 3.6 %convert_multiply_fusion = f32[1,1,128,32,384]{2,3,4,1,0:T(8,128)} fusion(bf16[1,1,128,32,384]{2,3,4,1,0:T(8,128)(2,1)S(1)} %copy.62), kind=kLoop, calls=%fused_computation.5 | loop fusion | flops 3145728 | bytes 9437184 | tf_op jit(solution)/shard_map/mul | solution.py:36
  29.1 0.0 copy-done.3
  29.1 0.0 copy-start
  29.1 0.0 copy-start.1
  29.2 0.0 copy-done.4
  29.2 0.1 fusion.33
  29.2 0.1 reshape.74
  29.4 3.7 %multiply_reduce_fusion = f32[128,32,32]{0,1,2:T(8,128)S(1)} fusion(f32[128,32,32,12]{0,1,3,2:T(8,128)} %bitcast.43, f32[128,12]{0,1:T(8,128)S(1)} %bitcast.44), kind=kLoop, calls=%fused_computation.4 | loop fusion | flops 3014656 | bytes 6821888 | tf_op jit(solution)/shard_map/reduce_sum | solution.py:37
  33.0 0.0 copy-done.2
  33.1 1.6 %copy.63 = bf16[128,32,32]{2,1,0:T(8,128)(2,1)S(1)} copy(bf16[128,32,32]{0,1,2:T(8,128)(2,1)S(1)} %multiply_convert_fusion) | data formatting | bytes 524288 | tf_op jit(solution)/shard_map/convert_element_type | solution.py:38
  34.8 0.0 copy-done
  34.8 0.0 copy-done.1
  34.8 0.1 copy.61
  34.9 0.7 gather_fusion
  35.7 1.4 fusion
  37.0 0.0 all-to-all-done.1
  37.0 12.1 %all-to-all-start = ((bf16[3,32,128]{1,0,2:T(4,128)(2,1)}), bf16[3,32,128]{1,0,2:T(4,128)(2,1)S(1)}, u32[]{:S(2)}, u32[]{:S(2)}) async-start(bf16[3,32,128]{1,0,2:T(4,128)(2,1)} %fusion), calls=%async_computation | async-start | bytes 262144 | tf_op jit(solution)/shard_map/all_to_all | solution.py:47
  49.2 0.7 reduce.7
  49.8 0.1 eq.15
  50.0 10.7 %all-to-all-done = bf16[3,32,128]{1,0,2:T(4,128)(2,1)S(1)} async-done(((bf16[3,32,128]{1,0,2:T(4,128)(2,1)}), bf16[3,32,128]{1,0,2:T(4,128)(2,1)S(1)}, u32[]{:S(2)}, u32[]{:S(2)}) %all-to-all-start) | async-done | bytes 24608 | tf_op jit(solution)/shard_map/all_to_all | solution.py:47
  60.7 0.2 convolution_convert_fusion.7
  61.0 12.7 %all_to_all.49 = bf16[8,3,32,128]{3,2,1,0:T(8,128)(2,1)S(1)} all-to-all(bf16[8,3,32,128]{3,2,1,0:T(8,128)(2,1)S(1)} %broadcast_in_dim.17), channel_id=1, replica_groups=mesh['pb'=8,'ka'=64] {'pb'}, dimensions={0} | all-to-all | bytes 393216 | tf_op jit(solution)/shard_map/all_to_all | solution.py:13
  73.7 0.1 copy.66
  73.9 0.7 gather_fusion.1
  74.6 0.7 fusion.1
  75.3 15.3 %all_to_all.50 = bf16[3,32,128]{1,0,2:T(4,128)(2,1)S(1)} all-to-all(bf16[3,32,128]{1,0,2:T(4,128)(2,1)S(1)} %fusion.1), channel_id=1, replica_groups=mesh['pb'=8,'ka'=64] {'ka'}, dimensions={2} | all-to-all | bytes 49152 | tf_op jit(solution)/shard_map/all_to_all | solution.py:47
  90.6 0.2 convolution_convert_fusion.6
  90.9 10.4 %all_to_all.51 = bf16[8,3,32,128]{3,2,1,0:T(8,128)(2,1)S(1)} all-to-all(bf16[8,3,32,128]{3,2,1,0:T(8,128)(2,1)S(1)} %broadcast_in_dim.18), channel_id=1, replica_groups=mesh['pb'=8,'ka'=64] {'pb'}, dimensions={0} | all-to-all | bytes 393216 | tf_op jit(solution)/shard_map/all_to_all | solution.py:13
  101.3 0.1 copy.69
  101.5 0.7 gather_fusion.2
  102.2 0.7 fusion.2
  102.9 15.3 %all_to_all.52 = bf16[3,32,128]{1,0,2:T(4,128)(2,1)S(1)} all-to-all(bf16[3,32,128]{1,0,2:T(4,128)(2,1)S(1)} %fusion.2), channel_id=1, replica_groups=mesh['pb'=8,'ka'=64] {'ka'}, dimensions={2} | all-to-all | bytes 49152 | tf_op jit(solution)/shard_map/all_to_all | solution.py:47
  118.3 0.2 convolution_convert_fusion.5
  118.5 10.4 %all_to_all.53 = bf16[8,3,32,128]{3,2,1,0:T(8,128)(2,1)S(1)} all-to-all(bf16[8,3,32,128]{3,2,1,0:T(8,128)(2,1)S(1)} %broadcast_in_dim.19), channel_id=1, replica_groups=mesh['pb'=8,'ka'=64] {'pb'}, dimensions={0} | all-to-all | bytes 393216 | tf_op jit(solution)/shard_map/all_to_all | solution.py:13
  128.9 0.1 copy.72
  129.1 0.7 gather_fusion.3
  129.8 0.7 fusion.3
  130.5 15.3 %all_to_all.54 = bf16[3,32,128]{1,0,2:T(4,128)(2,1)S(1)} all-to-all(bf16[3,32,128]{1,0,2:T(4,128)(2,1)S(1)} %fusion.3), channel_id=1, replica_groups=mesh['pb'=8,'ka'=64] {'ka'}, dimensions={2} | all-to-all | bytes 49152 | tf_op jit(solution)/shard_map/all_to_all | solution.py:47
  145.9 0.2 convolution_convert_fusion.4
  146.1 10.4 %all_to_all.55 = bf16[8,3,32,128]{3,2,1,0:T(8,128)(2,1)S(1)} all-to-all(bf16[8,3,32,128]{3,2,1,0:T(8,128)(2,1)S(1)} %broadcast_in_dim.34), channel_id=1, replica_groups=mesh['pb'=8,'ka'=64] {'pb'}, dimensions={0} | all-to-all | bytes 393216 | tf_op jit(solution)/shard_map/all_to_all | solution.py:13
  156.5 0.6 add_multiply_fusion
  (16 shorter events, 0.4 us)
Async XLA Ops:
  2.5 34.5 %all-to-all-start.1 = ((s32[64,2,1]{1,2,0:T(1,128)}), s32[64,2,1]{1,2,0:T(1,128)S(1)}, u32[]{:S(2)}, u32[]{:S(2)}) async-start(s32[64,2,1]{1,2,0:T(1,128)} %bitcast.6), calls=%async_computation.1 | async-start | bytes 65536 | tf_op jit(solution)/shard_map/all_to_all | solution.py:39
  21.0 8.2 %copy-start.3 = (f32[1,1,128,12]{2,1,3,0:T(1,128)S(1)}, f32[1,1,128,12]{2,1,3,0:T(1,128)}, u32[]{:S(2)}) copy-start(f32[1,1,128,12]{2,1,3,0:T(1,128)} %param.11) | copy-start | bytes 18436
  25.6 3.6 %copy-start.4 = (s32[1,1,64]{2,1,0:T(1,128)S(1)}, s32[1,1,64]{2,1,0:T(1,128)}, u32[]{:S(2)}) copy-start(s32[1,1,64]{2,1,0:T(1,128)} %param.13) | copy-start | bytes 772
  25.6 7.5 %copy-start.2 = (s32[1,1,128,32]{2,3,1,0:T(8,128)S(1)}, s32[1,1,128,32]{2,3,1,0:T(8,128)}, u32[]{:S(2)}) copy-start(s32[1,1,128,32]{2,3,1,0:T(8,128)} %param.12) | copy-start | bytes 49156
  29.1 5.6 %copy-start = (f32[3,32,128]{2,1,0:T(8,128)S(1)}, f32[3,32,128]{2,1,0:T(8,128)}, u32[]{:S(2)}) copy-start(f32[3,32,128]{2,1,0:T(8,128)} %param.16) | copy-start | bytes 147460
  29.1 5.6 %copy-start.1 = (f32[32,128]{1,0:T(8,128)S(1)}, f32[32,128]{1,0:T(8,128)}, u32[]{:S(2)}) copy-start(f32[32,128]{1,0:T(8,128)} %param.17) | copy-start | bytes 49156
  37.0 23.7 %all-to-all-start = ((bf16[3,32,128]{1,0,2:T(4,128)(2,1)}), bf16[3,32,128]{1,0,2:T(4,128)(2,1)S(1)}, u32[]{:S(2)}, u32[]{:S(2)}) async-start(bf16[3,32,128]{1,0,2:T(4,128)(2,1)} %fusion), calls=%async_computation | async-start | bytes 262144 | tf_op jit(solution)/shard_map/all_to_all | solution.py:47
where the time goes:
time: 158 us; the launch traced here: 157 us
  blocking collectives  89.8 us (57%)
  starting transfers between devices  29.3 us (19%)
  local copies, waits for them, and re-layouts  11.4 us (7%)
  other arithmetic  11.4 us (7%)
  waiting for transfers between devices  10.7 us (7%)
  matrix products  4.34 us (3%)
    all_to_all x3, blocking collectives, shards(): lax.all_to_all(local_terms.astype(jnp.bfloat16), 'ka', split_axis=2, conc...  46 us
    all_to_all x4, blocking collectives, from_everyone(): return lax.all_to_all(copies, axis, split_axis=0, concat_axis=0, tiled=True)  43.8 us
    all_to_all x1, starting transfers between devices, shards(): lax.all_to_all(k_target[0, 0], 'ka', split_axis=0, concat_axis=0, tiled=T...  17.1 us
    all_to_all x1, starting transfers between devices, shards(): lax.all_to_all(local_terms.astype(jnp.bfloat16), 'ka', split_axis=2, conc...  12.1 us
    all_to_all x1, waiting for transfers between devices, shards(): lax.all_to_all(local_terms.astype(jnp.bfloat16), 'ka', split_axis=2, conc...  10.7 us
    unnamed x13, local copies, waits for them, and re-layouts  5.12 us
    reduce_sum x1, other arithmetic, shards(): summed = jnp.sum(squared * phonon_occ[0, 0][:, None, None, :], axis=3)  3.66 us
    mul x1, other arithmetic, shards(): widened * widened  3.56 us
  transfers between devices with their start and end apart: 2, of which 1 were waited for; matrix products, arithmetic and copies ran while one was open for 11% of the time, Pallas kernels for 0%

commit v1 on v0

v1 whole, which is shorter than its diff:
```python
import jax
import jax.numpy as jnp
from jax import lax
from jax.experimental import pallas as pl
from jax.experimental.pallas import tpu as pltpu
from jax.sharding import PartitionSpec as P

MODES = 12
TILE_SLOTS = 2
ITERS = 4
BANDS = 32
ROWS = 3 * BANDS
TILES = 128
LANES = BANDS * MODES
CHUNKS = 8
F32 = jnp.float32
BF16 = jnp.bfloat16


def iota(shape, axis):
    return lax.broadcasted_iota(jnp.int32, shape, axis)


def updated(velocity, lifetime, scattering):
    parts = []
    for i in range(3):
        rows = slice(i * BANDS, (i + 1) * BANDS)
        total = velocity[rows, :]
        if scattering is not None:
            total = total + scattering[rows, :]
        parts.append(lifetime * total)
    return jnp.concatenate(parts, axis=0)


def send_terms(deviation, weight_ref, source_ref, target_ref, chosen_ref, term_ref, out_ref):
    picks = (iota((TILES, TILES), 0) == source_ref[...]).astype(F32).astype(BF16)
    chosen_ref[...] = jnp.dot(deviation.astype(BF16), picks, preferred_element_type=F32)
    for i in range(3):
        total = None
        for m in range(BANDS):
            term = weight_ref[pl.ds(m * BANDS, BANDS), :] * chosen_ref[pl.ds(i * BANDS + m, 1), :]
            total = term if total is None else total + term
        term_ref[pl.ds(i * BANDS, BANDS), :] = total
    tail = jnp.where(iota((BANDS, TILES), 0) == 0, target_ref[...].astype(F32), 0.0)
    term_ref[pl.ds(ROWS, BANDS), :] = tail
    out_ref[...] = term_ref[...].T.astype(BF16)


def weight_kernel(
    coupling_hbm, occ_ref, window_ref, count_ref, source_ref, target_ref, velocity_ref, lifetime_ref,
    weight_ref, out_ref,
    tiles, flat, occ_wide, occ_pad, chosen_ref, term_ref, sems,
):
    step = TILES // CHUNKS
    copies = []
    for c in range(CHUNKS):
        part = pl.ds(c * step, step)
        copies.append(pltpu.make_async_copy(coupling_hbm.at[part], tiles.at[part], sems.at[c]))
        copies[-1].start()
    occ_pad[...] = jnp.zeros_like(occ_pad)
    occ_pad[pl.ds(0, MODES), :] = occ_ref[...]
    spread = (iota((16, LANES), 1) % MODES == iota((16, LANES), 0)).astype(F32)
    occ_wide[...] = lax.dot_general(
        occ_pad[...].T, spread, (((1,), (0,)), ((), ())),
        precision=lax.Precision.HIGHEST, preferred_element_type=F32,
    )
    gather = (iota((LANES, TILES), 0) // MODES == iota((LANES, TILES), 1) % BANDS).astype(F32).astype(BF16)
    group = iota((1, 1, TILES), 2) // BANDS
    for c in range(CHUNKS):
        copies[c].wait()
        part = tiles[pl.ds(c * step, step)]
        occ = occ_wide[pl.ds(c * step, step), :].astype(BF16)
        scaled = part * part * occ[:, None, :]
        summed = jnp.dot(
            scaled.reshape(step * BANDS, LANES), gather, preferred_element_type=F32
        ).reshape(step, 4, 8, TILES)
        merged = summed[:, 0]
        for j in range(1, 4):
            merged = jnp.where(group == j, summed[:, j], merged)
        flat[pl.ds(c * step * 8, step * 8), :] = merged.reshape(step * 8, TILES)
    count = count_ref[...].astype(F32).astype(BF16)
    owner = (iota((64, TILES), 1) // TILE_SLOTS == iota((64, TILES), 0)).astype(F32).astype(BF16)
    live = jnp.dot(jnp.broadcast_to(count, (8, 64)), owner, preferred_element_type=F32)
    slot = (iota((8, TILES), 1) % TILE_SLOTS).astype(F32)
    live = (slot < live).astype(F32)
    mask = window_ref[...].astype(F32) * live[0:1, :]
    for q in range(8):
        turned = flat[pl.ds(q, TILES, stride=8), :].T
        for j in range(4):
            n = j * 8 + q
            weight_ref[pl.ds(n, BANDS, stride=BANDS), :] = (
                turned[j * BANDS : (j + 1) * BANDS, :] * mask[n : n + 1, :]
            )
    deviation = updated(velocity_ref[...], lifetime_ref[...], None)
    send_terms(deviation, weight_ref, source_ref, target_ref, chosen_ref, term_ref, out_ref)


def step_kernel(
    parts_ref, weight_ref, source_ref, target_ref, velocity_ref, lifetime_ref, out_ref, chosen_ref, term_ref
):
    deviation = updated(velocity_ref[...], lifetime_ref[...], sum_parts(parts_ref))
    send_terms(deviation, weight_ref, source_ref, target_ref, chosen_ref, term_ref, out_ref)


def sum_parts(parts_ref):
    total = parts_ref[0].astype(F32)
    for p in range(1, parts_ref.shape[0]):
        total = total + parts_ref[p].astype(F32)
    return total


def final_kernel(parts_ref, velocity_ref, lifetime_ref, out_ref):
    out_ref[...] = updated(velocity_ref[...], lifetime_ref[...], sum_parts(parts_ref))


def receive_kernel(terms_ref, out_ref):
    terms = terms_ref[...].astype(F32)
    target = terms[:, ROWS : ROWS + 1].astype(jnp.int32)
    onehot = (iota((TILES, TILES), 1) == target).astype(F32).astype(BF16)
    turned = terms.T[:ROWS, :].astype(BF16)
    partial_sum = jnp.dot(turned, onehot, preferred_element_type=F32).astype(BF16)
    for p in range(out_ref.shape[0]):
        out_ref[p] = partial_sum


VMEM = pl.BlockSpec(memory_space=pltpu.VMEM)


def call(body, name, ins, outs, scratch=(), limit=4 << 20, flops=1000000):
    return pl.pallas_call(
        body,
        name=name,
        in_specs=ins,
        out_specs=[VMEM] * len(outs),
        out_shape=[jax.ShapeDtypeStruct(s, d) for s, d in outs],
        scratch_shapes=list(scratch),
        compiler_params=pltpu.CompilerParams(vmem_limit_bytes=limit),
        cost_estimate=pl.CostEstimate(flops=flops, bytes_accessed=1 << 20, transcendentals=0),
    )


def shards(coupling, phonon_occ, band_window, pair_count, k_target, kq_source, velocity, lifetime):
    groups = lax.axis_size("pb")
    small = [pltpu.VMEM((ROWS, TILES), F32), pltpu.VMEM((TILES, TILES), F32)]
    velocity = velocity.reshape(ROWS, TILES)
    source = kq_source.reshape(1, TILES)
    target = k_target.reshape(1, TILES)
    weight, terms = call(
        weight_kernel, "weights", [pl.BlockSpec(memory_space=pl.ANY)] + [VMEM] * 7,
        [((BANDS * BANDS, TILES), F32), ((TILES, TILES), BF16)],
        [
            pltpu.VMEM((TILES, BANDS, LANES), BF16),
            pltpu.VMEM((TILES * 8, TILES), F32),
            pltpu.VMEM((TILES, LANES), F32),
            pltpu.VMEM((16, TILES), F32),
            *small,
            pltpu.SemaphoreType.DMA((CHUNKS,)),
        ],
        limit=16 << 20,
    )(
        coupling[0, 0], phonon_occ[0, 0].T, band_window[0, 0].T, pair_count[0], source, target, velocity, lifetime,
    )
    for iteration in range(ITERS):
        if iteration:
            (terms,) = call(step_kernel, "step", [VMEM] * 6, [((TILES, TILES), BF16)], small)(
                parts, weight, source, target, velocity, lifetime
            )
        arrived = lax.all_to_all(
            terms.reshape(-1, TILE_SLOTS, TILES), "ka", split_axis=0, concat_axis=0, tiled=True
        ).reshape(TILES, TILES)
        (copies,) = call(receive_kernel, "receive", [VMEM], [((groups, ROWS, TILES), BF16)])(arrived)
        parts = lax.all_to_all(copies, "pb", split_axis=0, concat_axis=0, tiled=True)
    (deviation,) = call(final_kernel, "final", [VMEM] * 3, [((ROWS, TILES), F32)])(
        parts, velocity, lifetime
    )
    return deviation.reshape(3, BANDS, TILES)


def solution(mesh):
    placed = (
        P("pb", "ka", None, None, None),
        P("pb", "ka", None, None),
        P("pb", "ka", None, None),
        P("pb", "ka", None),
        P("pb", "ka", None),
        P("pb", "ka", None),
        P(None, None, "ka"),
        P(None, "ka"),
    )
    return jax.shard_map(
        shards, mesh=mesh, in_specs=placed, out_specs=P(None, None, "ka"), check_vma=False
    )
```

time: 158 us -> 130 us (0.82)
  starting transfers between devices: 29.3 us -> 0 us
  blocking collectives: 89.8 us -> 115 us
  other arithmetic: 11.4 us -> 0 us
  waiting for transfers between devices: 10.7 us -> 0 us
  Pallas kernels: 0 us -> 7.68 us
  local copies, waits for them, and re-layouts: 11.4 us -> 6.78 us
  matrix products: 4.34 us -> 0 us
    all_to_all x2 -> x0, starting transfers between devices: 29.3 us -> none  [the longest x1 17.1 us: shards(): lax.all_to_all(k_target[0, 0], 'ka', split_axis=0, concat_axis=0, tiled=T...]
    all_to_all x7 -> x8, blocking collectives: 89.8 us -> 115 us  [the longest x4 71.8 us: shards(): lax.all_to_all(terms.reshape(-1, TILE_SLOTS, TILES), 'ka', split_axis=0,...]
    all_to_all x2 -> x0, waiting for transfers between devices: 10.7 us -> none  [the longest x1 10.7 us: shards(): lax.all_to_all(local_terms.astype(jnp.bfloat16), 'ka', split_axis=2, conc...]
    pallas_call x0 -> x9, Pallas kernels: none -> 7.68 us  [the longest x1 4.99 us: shards(): call(weight_kernel, 'weights', [pl.BlockSpec(memory_space=pl.ANY)] + [VME...]
    dot_general x8 -> x0, matrix products: 4.34 us -> none  [the longest x4 3.49 us: tile_terms(): jnp.einsum('tnm,dmt->dnt', weight, chosen, preferred_element_type=jnp.flo...]
    mul x3 -> x0, other arithmetic: 4.2 us -> none  [the longest x1 3.56 us: shards(): widened * widened]
    reduce_sum x5 -> x0, other arithmetic: 3.78 us -> none  [the longest x1 3.66 us: shards(): summed = jnp.sum(squared * phonon_occ[0, 0][:, None, None, :], axis=3)]
    gather x4 -> x0, local copies, waits for them, and re-layouts: 2.97 us -> none  [shards(): local_terms = tile_terms(weight, jnp.take(rounded, kq_source[0, 0], axis=2))]
  transfers between devices with their start and end apart: 2 -> 0, of which waited for: 1 -> 0; matrix products, arithmetic and copies ran while one was open for 11% -> 0% of each run, Pallas kernels for 0% -> 0%
where the time goes in v1:
time: 130 us; the launch traced here: 129 us
  blocking collectives  115 us (88%)
  Pallas kernels  7.68 us (6%)
  local copies, waits for them, and re-layouts  6.78 us (5%)
    all_to_all x4, blocking collectives, shards(): lax.all_to_all(terms.reshape(-1, TILE_SLOTS, TILES), 'ka', split_axis=0,...  71.8 us
    all_to_all x4, blocking collectives, shards(): lax.all_to_all(copies, 'pb', split_axis=0, concat_axis=0, tiled=True)  43.1 us
    unnamed x15, local copies, waits for them, and re-layouts  6.78 us
    pallas_call x1, Pallas kernels, shards(): call(weight_kernel, 'weights', [pl.BlockSpec(memory_space=pl.ANY)] + [VME...  4.99 us

profile of v1, /device:TPU:1, one launch (start us, length us, event | category | flops | bytes accessed | tf_op | source)
XLA Modules:
  0.0 129.4 jit_solution(14524297527250642790)
XLA Ops:
  0.0 0.7 copy.11
  0.7 0.0 copy-start
  0.7 1.9 %copy-done = bf16[1,1,128,32,384]{4,3,2,1,0:T(8,128)(2,1)S(1)} copy-done((bf16[1,1,128,32,384]{4,3,2,1,0:T(8,128)(2,1)S(1)}, bf16[1,1,128,32,384]{4,3,2,1,0:T(8,128)(2,1)}, u32[]{:S(2)}) %copy-start) | copy-done | bytes 3145752
  2.6 0.0 copy-start.1
  2.6 0.8 copy-done.1
  3.4 0.0 copy-start.2
  3.4 0.7 copy-done.2
  4.1 0.0 copy-start.3
  4.1 0.7 copy-done.3
  4.8 0.0 copy-start.4
  4.8 0.7 copy-done.4
  5.5 0.0 copy-start.5
  5.5 0.7 copy-done.5
  6.1 0.0 copy-start.6
  6.1 0.7 copy-done.6
  6.8 5.0 %weights.1 = (f32[1024,128]{1,0:T(8,128)S(1)}, bf16[128,128]{1,0:T(8,128)(2,1)S(1)}) custom-call(bf16[128,32,384]{2,1,0:T(8,128)(2,1)S(1)} %bitcast.22, f32[12,128]{1,0:T(8,128)S(1)} %bitcast.35, s32[32,128]{1,0:T(8,128)S(1)} %bitcast.37, s32[1,64]{1,0:T(1,128)S(1)} %bitcast.46, s32[1,128]{1,0:T(1,128)S(1)} %bitcast.38, s32[1,128]{1,0:T(1,128)S(1)} %bitcast.42, ...), custom_call_target="tpu_custom_call" | custom-call | flops 1000000 | bytes 1048576 | tf_op jit(solution)/shard_map/weights/pallas_call | solution.py:148
  11.8 27.8 %all_to_all.40 = bf16[64,2,128]{2,1,0:T(2,128)(2,1)S(1)} all-to-all(bf16[64,2,128]{2,1,0:T(2,128)(2,1)S(1)} %bitcast.36), channel_id=1, replica_groups=mesh['pb'=8,'ka'=64] {'ka'}, dimensions={0} | all-to-all | bytes 65536 | tf_op jit(solution)/shard_map/all_to_all | solution.py:168
  39.6 0.2 receive.4
  39.8 12.1 %all_to_all.41.parts_ref = bf16[8,96,128]{2,1,0:T(8,128)(2,1)S(1)} all-to-all(bf16[8,96,128]{2,1,0:T(8,128)(2,1)S(1)} %receive.4), channel_id=1, replica_groups=mesh['pb'=8,'ka'=64] {'pb'}, dimensions={0} | all-to-all | bytes 393216 | tf_op jit(solution)/shard_map/all_to_all | solution.py:172
  51.9 0.4 step.3
  52.2 14.7 %all_to_all.42 = bf16[64,2,128]{2,1,0:T(2,128)(2,1)S(1)} all-to-all(bf16[64,2,128]{2,1,0:T(2,128)(2,1)S(1)} %bitcast.30), channel_id=1, replica_groups=mesh['pb'=8,'ka'=64] {'ka'}, dimensions={0} | all-to-all | bytes 65536 | tf_op jit(solution)/shard_map/all_to_all | solution.py:168
  66.9 0.2 receive.5
  67.2 10.4 %all_to_all.43.parts_ref = bf16[8,96,128]{2,1,0:T(8,128)(2,1)S(1)} all-to-all(bf16[8,96,128]{2,1,0:T(8,128)(2,1)S(1)} %receive.5), channel_id=1, replica_groups=mesh['pb'=8,'ka'=64] {'pb'}, dimensions={0} | all-to-all | bytes 393216 | tf_op jit(solution)/shard_map/all_to_all | solution.py:172
  77.5 0.4 step.4
  77.9 14.7 %all_to_all.44 = bf16[64,2,128]{2,1,0:T(2,128)(2,1)S(1)} all-to-all(bf16[64,2,128]{2,1,0:T(2,128)(2,1)S(1)} %bitcast.32), channel_id=1, replica_groups=mesh['pb'=8,'ka'=64] {'ka'}, dimensions={0} | all-to-all | bytes 65536 | tf_op jit(solution)/shard_map/all_to_all | solution.py:168
  92.5 0.2 receive.6
  92.8 10.4 %all_to_all.45.parts_ref = bf16[8,96,128]{2,1,0:T(8,128)(2,1)S(1)} all-to-all(bf16[8,96,128]{2,1,0:T(8,128)(2,1)S(1)} %receive.6), channel_id=1, replica_groups=mesh['pb'=8,'ka'=64] {'pb'}, dimensions={0} | all-to-all | bytes 393216 | tf_op jit(solution)/shard_map/all_to_all | solution.py:172
  103.2 0.4 step.5
  103.5 14.7 %all_to_all.46 = bf16[64,2,128]{2,1,0:T(2,128)(2,1)S(1)} all-to-all(bf16[64,2,128]{2,1,0:T(2,128)(2,1)S(1)} %bitcast.28), channel_id=1, replica_groups=mesh['pb'=8,'ka'=64] {'ka'}, dimensions={0} | all-to-all | bytes 65536 | tf_op jit(solution)/shard_map/all_to_all | solution.py:168
  118.2 0.2 receive.7
  118.4 10.4 %all_to_all.47.parts_ref = bf16[8,96,128]{2,1,0:T(8,128)(2,1)S(1)} all-to-all(bf16[8,96,128]{2,1,0:T(8,128)(2,1)S(1)} %receive.7), channel_id=1, replica_groups=mesh['pb'=8,'ka'=64] {'pb'}, dimensions={0} | all-to-all | bytes 393216 | tf_op jit(solution)/shard_map/all_to_all | solution.py:172
  128.8 0.7 final.1
Async XLA Ops:
  0.7 1.9 %copy-start = (bf16[1,1,128,32,384]{4,3,2,1,0:T(8,128)(2,1)S(1)}, bf16[1,1,128,32,384]{4,3,2,1,0:T(8,128)(2,1)}, u32[]{:S(2)}) copy-start(bf16[1,1,128,32,384]{4,3,2,1,0:T(8,128)(2,1)} %param.8) | copy-start | bytes 9437188
  2.6 0.8 copy-start.1
  3.4 0.7 copy-start.2
  4.1 0.7 copy-start.3
  4.8 0.7 copy-start.4
  5.5 0.7 copy-start.5
  6.1 0.7 copy-start.6

commit v2 on v1

v2 whole, which is shorter than its diff:
```python
import jax
import jax.numpy as jnp
from jax import lax
from jax.experimental import pallas as pl
from jax.experimental.pallas import tpu as pltpu
from jax.sharding import PartitionSpec as P

MODES = 12
TILE_SLOTS = 2
ITERS = 4
BANDS = 32
ROWS = 3 * BANDS
TILES = 128
LANES = BANDS * MODES
CHUNKS = 8
F32 = jnp.float32
BF16 = jnp.bfloat16


def iota(shape, axis):
    return lax.broadcasted_iota(jnp.int32, shape, axis)


def updated(state_ref, scattering):
    lifetime = state_ref[pl.ds(ROWS, BANDS), :]
    parts = []
    for i in range(3):
        rows = slice(i * BANDS, (i + 1) * BANDS)
        total = state_ref[rows, :]
        if scattering is not None:
            total = total + scattering[rows, :]
        parts.append(lifetime * total)
    return jnp.concatenate(parts, axis=0)


def send_terms(deviation, weight_ref, index_ref, chosen_ref, half_ref, term_ref, out_ref):
    picks = (iota((TILES, TILES), 0) == index_ref[0:1, :]).astype(F32).astype(BF16)
    chosen_ref[...] = jnp.dot(deviation.astype(BF16), picks, preferred_element_type=F32)
    first = iota((8, TILES), 0) < 4
    for i in range(3):
        pairs = []
        for m in range(0, BANDS, 2):
            row = i * BANDS + m
            low = jnp.broadcast_to(chosen_ref[pl.ds(row, 1), :], (8, TILES))
            high = jnp.broadcast_to(chosen_ref[pl.ds(row + 1, 1), :], (8, TILES))
            pairs.append(jnp.where(first, low, high))
        for q in range(8):
            total = None
            for m, pair in enumerate(pairs):
                term = weight_ref[pl.ds(q * TILES + m * 8, 8), :] * pair
                total = term if total is None else total + term
            half_ref[pl.ds(i * 64 + q * 8, 8), :] = total
        for j in range(4):
            term_ref[pl.ds(i * BANDS + j * 8, 8), :] = (
                half_ref[pl.ds(i * 64 + j, 8, stride=8), :]
                + half_ref[pl.ds(i * 64 + j + 4, 8, stride=8), :]
            )
    target = index_ref[1:2, :].astype(F32)
    term_ref[pl.ds(ROWS, BANDS), :] = jnp.where(iota((BANDS, TILES), 0) == 0, target, 0.0)
    out_ref[...] = term_ref[...].T.astype(BF16)


def weight_kernel(
    coupling, occ, window, count, source, target, velocity, lifetime,
    weight_ref, out_ref, state_ref, index_ref,
    tiles, flat, occ_wide, occ_pad, window_ref, count_ref, mask_ref, chosen_ref, half_ref, term_ref, sems, small_sems,
):
    small = []
    for place, (origin, into) in enumerate((
        *((occ.at[v], occ_pad.at[pl.ds(v, 1)]) for v in range(MODES)),
        (count, count_ref),
        (window, window_ref),
        (velocity, state_ref.at[pl.ds(0, ROWS)]),
        (lifetime, state_ref.at[pl.ds(ROWS, BANDS)]),
        (source, index_ref.at[pl.ds(0, 1)]),
        (target, index_ref.at[pl.ds(1, 1)]),
    )):
        small.append(pltpu.make_async_copy(origin, into, small_sems.at[place]))
    for copy in small[:MODES]:
        copy.start()
    step = TILES // CHUNKS
    copies = []
    for c in range(CHUNKS):
        part = pl.ds(c * step, step)
        copies.append(pltpu.make_async_copy(coupling.at[part], tiles.at[part], sems.at[c]))
        copies[-1].start()
        if c == 0:
            for copy in small[MODES:]:
                copy.start()
    spread = (iota((16, LANES), 1) % MODES == iota((16, LANES), 0)).astype(F32).astype(BF16)
    gather = (iota((LANES, TILES), 0) // MODES == iota((LANES, TILES), 1) // 4).astype(F32).astype(BF16)
    group = iota((1, TILES), 1) % 4
    for copy in small[:MODES]:
        copy.wait()
    valid = iota((16, TILES), 0) < MODES
    occ_rows = jnp.where(valid, occ_pad[...], 0.0).T.astype(BF16)
    occ_wide[...] = jnp.dot(occ_rows, spread, preferred_element_type=F32)
    summed = None
    for c in range(CHUNKS + 1):
        before = summed
        if c < CHUNKS:
            copies[c].wait()
            rows = []
            for t in range(c * step, (c + 1) * step):
                tile = tiles[t]
                wide = jnp.broadcast_to(occ_wide[pl.ds(t, 1), :], (BANDS, LANES)).astype(BF16)
                rows.append(tile * tile * wide)
            summed = jnp.dot(jnp.concatenate(rows, axis=0), gather, preferred_element_type=F32)
        for t in range(step if c else 0):
            merged = before[t * BANDS : t * BANDS + 8, :]
            for j in range(1, 4):
                row = t * BANDS + j * 8
                merged = jnp.where(group == j, before[row : row + 8, :], merged)
            flat[pl.ds(((c - 1) * step + t) * 8, 8), :] = merged
    for copy in small[MODES:]:
        copy.wait()
    count = count_ref[...].astype(F32).astype(BF16)
    owner = (iota((64, TILES), 1) // TILE_SLOTS == iota((64, TILES), 0)).astype(F32).astype(BF16)
    live = jnp.dot(jnp.broadcast_to(count, (8, 64)), owner, preferred_element_type=F32)
    slot = (iota((8, TILES), 1) % TILE_SLOTS).astype(F32)
    live = (slot < live).astype(F32)
    mask = window_ref[...].astype(F32) * live[0:1, :]
    mask_ref[pl.ds(0, BANDS), :] = mask
    mask_ref[pl.ds(BANDS, BANDS), :] = mask
    for q in range(8):
        turned = flat[pl.ds(q, TILES, stride=8), :].T
        rows = mask_ref[pl.ds(q, 8, stride=8), :]
        for m in range(16):
            weight_ref[pl.ds(q * TILES + m * 8, 8), :] = turned[m * 8 : m * 8 + 8, :] * rows
    deviation = updated(state_ref, None)
    send_terms(deviation, weight_ref, index_ref, chosen_ref, half_ref, term_ref, out_ref)


def step_kernel(parts_ref, weight_ref, state_ref, index_ref, out_ref, chosen_ref, half_ref, term_ref):
    deviation = updated(state_ref, sum_parts(parts_ref))
    send_terms(deviation, weight_ref, index_ref, chosen_ref, half_ref, term_ref, out_ref)


def sum_parts(parts_ref):
    total = parts_ref[0].astype(F32)
    for p in range(1, parts_ref.shape[0]):
        total = total + parts_ref[p].astype(F32)
    return total


def final_kernel(parts_ref, state_ref, out_ref):
    out_ref[...] = updated(state_ref, sum_parts(parts_ref))


def receive_kernel(terms_ref, out_ref):
    terms = terms_ref[...].astype(F32)
    target = terms[:, ROWS : ROWS + 1].astype(jnp.int32)
    onehot = (iota((TILES, TILES), 1) == target).astype(F32).astype(BF16)
    turned = terms.T[:ROWS, :].astype(BF16)
    partial_sum = jnp.dot(turned, onehot, preferred_element_type=F32).astype(BF16)
    for p in range(out_ref.shape[0]):
        out_ref[p] = partial_sum


VMEM = pl.BlockSpec(memory_space=pltpu.VMEM)


def call(body, name, ins, outs, scratch=(), limit=4 << 20, flops=1000000):
    return pl.pallas_call(
        body,
        name=name,
        in_specs=ins,
        out_specs=[VMEM] * len(outs),
        out_shape=[jax.ShapeDtypeStruct(s, d) for s, d in outs],
        scratch_shapes=list(scratch),
        compiler_params=pltpu.CompilerParams(vmem_limit_bytes=limit),
        cost_estimate=pl.CostEstimate(flops=flops, bytes_accessed=1 << 20, transcendentals=0),
    )


def shards(coupling, phonon_occ, band_window, pair_count, k_target, kq_source, velocity, lifetime):
    groups = lax.axis_size("pb")
    small = [
        pltpu.VMEM((ROWS, TILES), F32), pltpu.VMEM((3 * 64, TILES), F32), pltpu.VMEM((TILES, TILES), F32)
    ]
    weight, terms, state, index = call(
        weight_kernel, "weights", [pl.BlockSpec(memory_space=pltpu.HBM)] * 8,
        [
            ((BANDS * BANDS, TILES), F32), ((TILES, TILES), BF16),
            ((TILES, TILES), F32), ((8, TILES), jnp.int32),
        ],
        [
            pltpu.VMEM((TILES, BANDS, LANES), BF16),
            pltpu.VMEM((TILES * 8, TILES), F32),
            pltpu.VMEM((TILES, LANES), F32),
            pltpu.VMEM((16, TILES), F32),
            pltpu.VMEM((BANDS, TILES), jnp.int32),
            pltpu.VMEM((1, 64), jnp.int32),
            pltpu.VMEM((2 * BANDS, TILES), F32),
            *small,
            pltpu.SemaphoreType.DMA((CHUNKS,)),
            pltpu.SemaphoreType.DMA((MODES + 6,)),
        ],
        limit=16 << 20,
    )(*(pltpu.with_memory_space_constraint(x, pltpu.HBM) for x in (
        coupling[0, 0], phonon_occ.transpose(0, 3, 1, 2).reshape(MODES, 1, TILES), band_window[0, 0].T, pair_count[0],
        kq_source.reshape(1, TILES), k_target.reshape(1, TILES), velocity.reshape(ROWS, TILES), lifetime,
    )))
    for iteration in range(ITERS):
        if iteration:
            (terms,) = call(step_kernel, "step", [VMEM] * 4, [((TILES, TILES), BF16)], small)(
                parts, weight, state, index
            )
        arrived = lax.all_to_all(
            terms.reshape(-1, TILE_SLOTS, TILES), "ka", split_axis=0, concat_axis=0, tiled=True
        ).reshape(TILES, TILES)
        (copies,) = call(receive_kernel, "receive", [VMEM], [((groups, ROWS, TILES), BF16)])(arrived)
        parts = lax.all_to_all(copies, "pb", split_axis=0, concat_axis=0, tiled=True)
    (deviation,) = call(final_kernel, "final", [VMEM] * 2, [((ROWS, TILES), F32)])(parts, state)
    return deviation.reshape(3, BANDS, TILES)


def solution(mesh):
    placed = (
        P("pb", "ka", None, None, None),
        P("pb", "ka", None, None),
        P("pb", "ka", None, None),
        P("pb", "ka", None),
        P("pb", "ka", None),
        P("pb", "ka", None),
        P(None, None, "ka"),
        P(None, "ka"),
    )
    return jax.shard_map(
        shards, mesh=mesh, in_specs=placed, out_specs=P(None, None, "ka"), check_vma=False
    )
```

time: 130 us -> 122 us (0.938)
  local copies, waits for them, and re-layouts: 6.78 us -> 0 us
    unnamed x15 -> x0, local copies, waits for them, and re-layouts: 6.78 us -> none
where the time goes in v2:
time: 122 us
  blocking collectives  115 us (94%)
  Pallas kernels  6.83 us (6%)
    all_to_all x4, blocking collectives, shards(): lax.all_to_all(terms.reshape(-1, TILE_SLOTS, TILES), 'ka', split_axis=0,...  71.8 us
    all_to_all x4, blocking collectives, shards(): lax.all_to_all(copies, 'pb', split_axis=0, concat_axis=0, tiled=True)  43.1 us
    pallas_call x1, Pallas kernels, shards(): call(weight_kernel, 'weights', [pl.BlockSpec(memory_space=pltpu.HBM)] * 8...  4.13 us

profile of v2, /device:TPU:1, one launch (start us, length us, event | category | flops | bytes accessed | tf_op | source)
XLA Modules:
  0.0 121.8 jit_solution(17836144189426702315)
XLA Ops:
  0.0 4.1 %weights.1 = (f32[1024,128]{1,0:T(8,128)S(1)}, bf16[128,128]{1,0:T(8,128)(2,1)S(1)}, f32[128,128]{1,0:T(8,128)S(1)}, s32[8,128]{1,0:T(8,128)S(1)}) custom-call(bf16[128,32,384]{2,1,0:T(8,128)(2,1)} %bitcast.28, f32[12,1,128]{2,1,0:T(1,128)} %bitcast.31, s32[32,128]{1,0:T(8,128)} %bitcast.30, s32[1,64]{1,0:T(1,128)} %bitcast.32, s32[1,128]{1,0:T(1,128)} %bitcast.33, ...), custom_call_target="tpu_custom_call" | custom-call | flops 1000000 | bytes 1048576 | tf_op jit(solution)/shard_map/weights/pallas_call | solution.py:181
  4.1 27.8 %all_to_all.40 = bf16[64,2,128]{2,1,0:T(2,128)(2,1)S(1)} all-to-all(bf16[64,2,128]{2,1,0:T(2,128)(2,1)S(1)} %bitcast.27), channel_id=1, replica_groups=mesh['pb'=8,'ka'=64] {'ka'}, dimensions={0} | all-to-all | bytes 65536 | tf_op jit(solution)/shard_map/all_to_all | solution.py:209
  31.9 0.2 receive.4
  32.2 12.1 %all_to_all.41.parts_ref = bf16[8,96,128]{2,1,0:T(8,128)(2,1)S(1)} all-to-all(bf16[8,96,128]{2,1,0:T(8,128)(2,1)S(1)} %receive.4), channel_id=1, replica_groups=mesh['pb'=8,'ka'=64] {'pb'}, dimensions={0} | all-to-all | bytes 393216 | tf_op jit(solution)/shard_map/all_to_all | solution.py:213
  44.2 0.4 step.3
  44.6 14.7 %all_to_all.42 = bf16[64,2,128]{2,1,0:T(2,128)(2,1)S(1)} all-to-all(bf16[64,2,128]{2,1,0:T(2,128)(2,1)S(1)} %bitcast.22), channel_id=1, replica_groups=mesh['pb'=8,'ka'=64] {'ka'}, dimensions={0} | all-to-all | bytes 65536 | tf_op jit(solution)/shard_map/all_to_all | solution.py:209
  59.3 0.2 receive.5
  59.5 10.4 %all_to_all.43.parts_ref = bf16[8,96,128]{2,1,0:T(8,128)(2,1)S(1)} all-to-all(bf16[8,96,128]{2,1,0:T(8,128)(2,1)S(1)} %receive.5), channel_id=1, replica_groups=mesh['pb'=8,'ka'=64] {'pb'}, dimensions={0} | all-to-all | bytes 393216 | tf_op jit(solution)/shard_map/all_to_all | solution.py:213
  69.9 0.4 step.4
  70.2 14.7 %all_to_all.44 = bf16[64,2,128]{2,1,0:T(2,128)(2,1)S(1)} all-to-all(bf16[64,2,128]{2,1,0:T(2,128)(2,1)S(1)} %bitcast.24), channel_id=1, replica_groups=mesh['pb'=8,'ka'=64] {'ka'}, dimensions={0} | all-to-all | bytes 65536 | tf_op jit(solution)/shard_map/all_to_all | solution.py:209
  84.9 0.2 receive.6
  85.2 10.4 %all_to_all.45.parts_ref = bf16[8,96,128]{2,1,0:T(8,128)(2,1)S(1)} all-to-all(bf16[8,96,128]{2,1,0:T(8,128)(2,1)S(1)} %receive.6), channel_id=1, replica_groups=mesh['pb'=8,'ka'=64] {'pb'}, dimensions={0} | all-to-all | bytes 393216 | tf_op jit(solution)/shard_map/all_to_all | solution.py:213
  95.5 0.4 step.5
  95.9 14.7 %all_to_all.46 = bf16[64,2,128]{2,1,0:T(2,128)(2,1)S(1)} all-to-all(bf16[64,2,128]{2,1,0:T(2,128)(2,1)S(1)} %bitcast.20), channel_id=1, replica_groups=mesh['pb'=8,'ka'=64] {'ka'}, dimensions={0} | all-to-all | bytes 65536 | tf_op jit(solution)/shard_map/all_to_all | solution.py:209
  110.6 0.2 receive.7
  110.8 10.4 %all_to_all.47.parts_ref = bf16[8,96,128]{2,1,0:T(8,128)(2,1)S(1)} all-to-all(bf16[8,96,128]{2,1,0:T(8,128)(2,1)S(1)} %receive.7), channel_id=1, replica_groups=mesh['pb'=8,'ka'=64] {'pb'}, dimensions={0} | all-to-all | bytes 393216 | tf_op jit(solution)/shard_map/all_to_all | solution.py:213
  121.2 0.7 final.1

commit v3 on v2

v3 whole, which is shorter than its diff:
```python
import jax
import jax.numpy as jnp
from jax import lax
from jax.experimental import pallas as pl
from jax.experimental.pallas import tpu as pltpu
from jax.sharding import PartitionSpec as P


MODES = 12
TILE_SLOTS = 2
ITERS = 4
BANDS = 32
ROWS = 3 * BANDS
TILES = 128
LANES = BANDS * MODES
CHUNKS = 8
WIDE = BANDS * BANDS
F32 = jnp.float32
BF16 = jnp.bfloat16


def iota(shape, axis):
    return lax.broadcasted_iota(jnp.int32, shape, axis)


def band_terms(weight, base, pairs, half_ref, term_ref, slot):
    for q in range(8):
        total = None
        for m, pair in enumerate(pairs):
            term = weight[pl.ds(q * TILES + m * 8, 8), :].astype(F32) * pair
            total = term if total is None else total + term
        half_ref[pl.ds(base + q * 8, 8), :] = total
    for j in range(4):
        term_ref[pl.ds(slot * BANDS + j * 8, 8), :] = (
            half_ref[pl.ds(base + j, 8, stride=8), :] + half_ref[pl.ds(base + j + 4, 8, stride=8), :]
        )


def band_pairs(chosen_ref, slot):
    first = iota((8, TILES), 0) < 4
    pairs = []
    for m in range(0, BANDS, 2):
        row = slot * BANDS + m
        low = jnp.broadcast_to(chosen_ref[pl.ds(row, 1), :], (8, TILES))
        high = jnp.broadcast_to(chosen_ref[pl.ds(row + 1, 1), :], (8, TILES))
        pairs.append(jnp.where(first, low, high))
    return pairs


def onehot(equal):
    return equal.astype(F32).astype(BF16)


def weight_kernel(
    coupling, occ, window, count, source, target, velocity, lifetime,
    wide_ref, out_ref, state_ref,
    weight_ref, index_ref, tiles, flat, occ_wide, occ_pad, window_ref, count_ref, mask_ref, chosen_ref, half_ref, term_ref, sems, small_sems,
):
    small = []
    for place, (origin, into) in enumerate((
        *((occ.at[v], occ_pad.at[pl.ds(v, 1)]) for v in range(MODES)),
        (count, count_ref),
        (window, window_ref),
        (velocity, state_ref.at[pl.ds(0, ROWS)]),
        (lifetime, state_ref.at[pl.ds(ROWS, BANDS)]),
        (source, index_ref.at[pl.ds(0, 1)]),
        (target, index_ref.at[pl.ds(1, 1)]),
    )):
        small.append(pltpu.make_async_copy(origin, into, small_sems.at[place]))
    for copy in small[:MODES]:
        copy.start()
    step = TILES // CHUNKS
    copies = []
    for c in range(CHUNKS):
        part = pl.ds(c * step, step)
        copies.append(pltpu.make_async_copy(coupling.at[part], tiles.at[part], sems.at[c]))
        copies[-1].start()
        if c == 0:
            for copy in small[MODES:]:
                copy.start()
    spread = (iota((16, LANES), 1) % MODES == iota((16, LANES), 0)).astype(F32).astype(BF16)
    gather = (iota((LANES, TILES), 0) // MODES == iota((LANES, TILES), 1) // 4).astype(F32).astype(BF16)
    group = iota((1, TILES), 1) % 4
    for copy in small[:MODES]:
        copy.wait()
    valid = iota((16, TILES), 0) < MODES
    occ_rows = jnp.where(valid, occ_pad[...], 0.0).T.astype(BF16)
    occ_wide[...] = jnp.dot(occ_rows, spread, preferred_element_type=F32)
    summed = None
    for c in range(CHUNKS + 1):
        before = summed
        if c < CHUNKS:
            copies[c].wait()
            rows = []
            for t in range(c * step, (c + 1) * step):
                tile = tiles[t]
                wide = jnp.broadcast_to(occ_wide[pl.ds(t, 1), :], (BANDS, LANES)).astype(BF16)
                rows.append(tile * tile * wide)
            summed = jnp.dot(jnp.concatenate(rows, axis=0), gather, preferred_element_type=F32)
        for t in range(step if c else 0):
            merged = before[t * BANDS : t * BANDS + 8, :]
            for j in range(1, 4):
                row = t * BANDS + j * 8
                merged = jnp.where(group == j, before[row : row + 8, :], merged)
            flat[pl.ds(((c - 1) * step + t) * 8, 8), :] = merged
    for copy in small[MODES:]:
        copy.wait()
    count = count_ref[...].astype(F32).astype(BF16)
    owner = (iota((64, TILES), 1) // TILE_SLOTS == iota((64, TILES), 0)).astype(F32).astype(BF16)
    live = jnp.dot(jnp.broadcast_to(count, (8, 64)), owner, preferred_element_type=F32)
    slot = (iota((8, TILES), 1) % TILE_SLOTS).astype(F32)
    live = (slot < live).astype(F32)
    mask = window_ref[...].astype(F32) * live[0:1, :]
    mask_ref[pl.ds(0, BANDS), :] = mask
    mask_ref[pl.ds(BANDS, BANDS), :] = mask
    for q in range(8):
        turned = flat[pl.ds(q, TILES, stride=8), :].T
        rows = mask_ref[pl.ds(q, 8, stride=8), :]
        for m in range(16):
            weight_ref[pl.ds(q * TILES + m * 8, 8), :] = turned[m * 8 : m * 8 + 8, :] * rows
    source_row = jnp.broadcast_to(index_ref[0:1, :], (16, TILES))
    wide_ref[pl.ds(0, WIDE), :] = weight_ref[...].astype(BF16)
    wide_ref[pl.ds(WIDE, 16), :] = source_row.astype(F32).astype(BF16)
    lifetime_now = state_ref[pl.ds(ROWS, BANDS), :]
    deviation = jnp.concatenate(
        [lifetime_now * state_ref[pl.ds(i * BANDS, BANDS), :] for i in range(3)], axis=0
    )
    picks = onehot(iota((TILES, TILES), 0) == index_ref[0:1, :])
    chosen_ref[...] = jnp.dot(deviation.astype(BF16), picks, preferred_element_type=F32)
    for i in range(3):
        band_terms(weight_ref, i * 64, band_pairs(chosen_ref, i), half_ref, term_ref, i)
    target = index_ref[1:2, :].astype(F32)
    term_ref[pl.ds(ROWS, BANDS), :] = jnp.where(iota((BANDS, TILES), 0) == 0, target, 0.0)
    out_ref[...] = term_ref[...].T.astype(BF16)


def receive_kernel(terms_ref, out_ref):
    terms = terms_ref[...].astype(F32)
    target = terms[:, ROWS : ROWS + 1].astype(jnp.int32)
    turned = terms.T
    places = onehot(iota((TILES, TILES), 1) == target)
    total = jnp.dot(turned[:ROWS, :].astype(BF16), places, preferred_element_type=F32)
    message = jnp.concatenate([total, turned[ROWS : ROWS + 8, :]], axis=0).astype(BF16)
    for p in range(out_ref.shape[0]):
        out_ref[p] = message


def direction_terms(deviation, weights, chosen_ref, half_ref, term_ref, out_ref):
    picks = []
    for weight in weights:
        source_row = weight[pl.ds(WIDE, 16), :].astype(F32)[0:1, :].astype(jnp.int32)
        picks.append(onehot(iota((TILES, TILES), 0) == source_row))
    chosen = jnp.dot(deviation.astype(BF16), jnp.concatenate(picks, axis=1), preferred_element_type=F32)
    for g, weight in enumerate(weights):
        chosen_ref[pl.ds(g * BANDS, BANDS), :] = chosen[:, g * TILES : (g + 1) * TILES]
    for g, weight in enumerate(weights):
        band_terms(weight, g * 64, band_pairs(chosen_ref, g), half_ref, term_ref, g)
    out_ref[...] = term_ref[...].T.astype(BF16)


def own_direction():
    return lax.axis_index("pb") // 2 % 3


def next_direction(state_ref, scattering):
    rows = pl.ds(pl.multiple_of(own_direction() * BANDS, BANDS), BANDS)
    return state_ref[pl.ds(ROWS, BANDS), :] * (state_ref[rows, :] + scattering)


def first_kernel(parts_ref, state_ref, w0, w1, w2, w3, out_ref, target_ref, chosen_ref, half_ref, term_ref):
    rows = pl.ds(pl.multiple_of(own_direction() * BANDS, BANDS), BANDS)
    total = parts_ref[0, rows, :].astype(F32)
    for p in range(1, parts_ref.shape[0]):
        total = total + parts_ref[p, rows, :].astype(F32)
    me = lax.axis_index("pb")
    groups = parts_ref.shape[0]
    for g in range(4):
        peer = lax.rem(me + groups - 2 * g, groups)
        target_ref[pl.ds(g, 1), :] = parts_ref[peer, pl.ds(ROWS, 8), :].astype(F32)[0:1, :]
    deviation = next_direction(state_ref, total)
    direction_terms(deviation, (w0, w1, w2, w3), chosen_ref, half_ref, term_ref, out_ref)


def step_kernel(mine_ref, other_ref, state_ref, w0, w1, w2, w3, out_ref, chosen_ref, half_ref, term_ref):
    deviation = next_direction(state_ref, mine_ref[...].astype(F32) + other_ref[...].astype(F32))
    direction_terms(deviation, (w0, w1, w2, w3), chosen_ref, half_ref, term_ref, out_ref)


def direction_sum(terms_ref, target_ref):
    turned = terms_ref[...].astype(F32).T.astype(BF16)
    left, right = [], []
    for g in range(4):
        target = target_ref[pl.ds(g, 1), :].astype(jnp.int32)
        right.append(onehot(iota((TILES, TILES), 0) == target))
        left.append(turned[g * BANDS : (g + 1) * BANDS, :])
    return lax.dot_general(
        jnp.concatenate(left, axis=1), jnp.concatenate(right, axis=1), (((1,), (1,)), ((), ())),
        preferred_element_type=F32,
    ).astype(BF16)


def sum_kernel(terms_ref, target_ref, out_ref):
    out_ref[...] = direction_sum(terms_ref, target_ref)


def last_sum_kernel(terms_ref, target_ref, out_ref):
    total = direction_sum(terms_ref, target_ref)
    for p in range(out_ref.shape[0]):
        out_ref[p] = total


def final_kernel(parts_ref, state_ref, out_ref):
    for i in range(3):
        total = parts_ref[2 * i].astype(F32) + parts_ref[2 * i + 1].astype(F32)
        rows = pl.ds(i * BANDS, BANDS)
        out_ref[rows, :] = state_ref[pl.ds(ROWS, BANDS), :] * (state_ref[rows, :] + total)


VMEM = pl.BlockSpec(memory_space=pltpu.VMEM)


def call(body, ins, outs, scratch=(), limit=4 << 20, flops=1000000):
    return pl.pallas_call(
        body,
        in_specs=ins,
        out_specs=[VMEM] * len(outs),
        out_shape=[jax.ShapeDtypeStruct(s, d) for s, d in outs],
        scratch_shapes=list(scratch),
        compiler_params=pltpu.CompilerParams(vmem_limit_bytes=limit),
        cost_estimate=pl.CostEstimate(flops=flops, bytes_accessed=1 << 20, transcendentals=0),
    )


def over_owners(terms):
    return lax.all_to_all(
        terms.reshape(-1, TILE_SLOTS, TILES), "ka", split_axis=0, concat_axis=0, tiled=True
    ).reshape(TILES, TILES)


def shards(coupling, phonon_occ, band_window, pair_count, k_target, kq_source, velocity, lifetime):
    groups = lax.axis_size("pb")
    small = [
        pltpu.VMEM((TILES, TILES), F32), pltpu.VMEM((4 * 64, TILES), F32), pltpu.VMEM((TILES, TILES), F32)
    ]
    wide, terms, state = call(
        weight_kernel, [pl.BlockSpec(memory_space=pltpu.HBM)] * 8,
        [((WIDE + 16, TILES), BF16), ((TILES, TILES), BF16), ((TILES, TILES), F32)],
        [
            pltpu.VMEM((WIDE, TILES), F32),
            pltpu.VMEM((8, TILES), jnp.int32),
            pltpu.VMEM((TILES, BANDS, LANES), BF16),
            pltpu.VMEM((TILES * 8, TILES), F32),
            pltpu.VMEM((TILES, LANES), F32),
            pltpu.VMEM((16, TILES), F32),
            pltpu.VMEM((BANDS, TILES), jnp.int32),
            pltpu.VMEM((1, 64), jnp.int32),
            pltpu.VMEM((2 * BANDS, TILES), F32),
            pltpu.VMEM((ROWS, TILES), F32), *small[1:],
            pltpu.SemaphoreType.DMA((CHUNKS,)),
            pltpu.SemaphoreType.DMA((MODES + 6,)),
        ],
        limit=16 << 20,
    )(*(pltpu.with_memory_space_constraint(x, pltpu.HBM) for x in (
        coupling[0, 0], phonon_occ.transpose(0, 3, 1, 2).reshape(MODES, 1, TILES), band_window[0, 0].T, pair_count[0],
        kq_source.reshape(1, TILES), k_target.reshape(1, TILES), velocity.reshape(ROWS, TILES), lifetime,
    )))
    arrived = over_owners(terms)
    weights = [wide]
    for shift in (1, 3, 2):
        weights.append(lax.ppermute(wide, "pb", [
            (p, (p + 2 * shift) % groups) for p in range(groups)
        ]))
    weights = [weights[0], weights[1], weights[3], weights[2]]
    (copies,) = call(receive_kernel, [VMEM], [((groups, ROWS + 8, TILES), BF16)])(arrived)
    parts = lax.all_to_all(copies, "pb", split_axis=0, concat_axis=0, tiled=True)
    terms, targets = call(
        first_kernel, [VMEM] * 6, [((TILES, TILES), BF16), ((8, TILES), F32)], small
    )(parts, state, *weights)
    for iteration in range(1, ITERS):
        if iteration > 1:
            other = lax.ppermute(mine, "pb", [(p, p + 1 - 2 * (p % 2)) for p in range(groups)])
            (terms,) = call(step_kernel, [VMEM] * 7, [((TILES, TILES), BF16)], small)(mine, other, state, *weights)
        arrived = over_owners(terms)
        if iteration < ITERS - 1:
            (mine,) = call(sum_kernel, [VMEM] * 2, [((BANDS, TILES), BF16)])(arrived, targets)
    (copies,) = call(last_sum_kernel, [VMEM] * 2, [((groups, BANDS, TILES), BF16)])(arrived, targets)
    parts = lax.all_to_all(copies, "pb", split_axis=0, concat_axis=0, tiled=True)
    (deviation,) = call(final_kernel, [VMEM] * 2, [((ROWS, TILES), F32)])(parts, state)
    return deviation.reshape(3, BANDS, TILES)


def solution(mesh):
    placed = (
        P("pb", "ka", None, None, None),
        P("pb", "ka", None, None),
        P("pb", "ka", None, None),
        P("pb", "ka", None),
        P("pb", "ka", None),
        P("pb", "ka", None),
        P(None, None, "ka"),
        P(None, "ka"),
    )
    return jax.shard_map(
        shards, mesh=mesh, in_specs=placed, out_specs=P(None, None, "ka"), check_vma=False
    )
```

time: 122 us -> 119 us (0.975)
  blocking collectives: 115 us -> 92.1 us
  starting transfers between devices: 0 us -> 17.6 us
  waiting for transfers between devices: 0 us -> 1.62 us
    all_to_all x4 -> x2, blocking collectives: 43.1 us -> 21.1 us  [shards(): lax.all_to_all(copies, 'pb', split_axis=0, concat_axis=0, tiled=True)]
    ppermute x0 -> x5, starting transfers between devices: none -> 17.6 us  [the longest x3 10.1 us: shards(): lax.ppermute(wide, 'pb', [(p, (p + 2 * shift) % groups) for p in range(gr...]
    ppermute x0 -> x5, waiting for transfers between devices: none -> 1.62 us  [the longest x2 1.61 us: shards(): lax.ppermute(mine, 'pb', [(p, p + 1 - 2 * (p % 2)) for p in range(groups)])]
  transfers between devices with their start and end apart: 0 -> 5, of which waited for: 0 -> 2; matrix products, arithmetic and copies ran while one was open for 0% -> 0% of each run, Pallas kernels for 0% -> 0%
where the time goes in v3:
time: 119 us; the launch traced here: 118 us
  blocking collectives  92.1 us (77%)
  starting transfers between devices  17.6 us (15%)
  Pallas kernels  6.98 us (6%)
  waiting for transfers between devices  1.62 us (1%)
    all_to_all x4, blocking collectives, over_owners(): lax.all_to_all(terms.reshape(-1, TILE_SLOTS, TILES), 'ka', split_axis=0,...  71 us
    all_to_all x2, blocking collectives, shards(): lax.all_to_all(copies, 'pb', split_axis=0, concat_axis=0, tiled=True)  21.1 us
    ppermute x3, starting transfers between devices, shards(): lax.ppermute(wide, 'pb', [(p, (p + 2 * shift) % groups) for p in range(gr...  10.1 us
    ppermute x2, starting transfers between devices, shards(): lax.ppermute(mine, 'pb', [(p, p + 1 - 2 * (p % 2)) for p in range(groups)])  7.43 us
    pallas_call x1, Pallas kernels, shards(): call(weight_kernel, [pl.BlockSpec(memory_space=pltpu.HBM)] * 8, [((WIDE +...  4.13 us
  transfers between devices with their start and end apart: 5, of which 2 were waited for; matrix products, arithmetic and copies ran while one was open for 0% of the time, Pallas kernels for 0%

profile of v3, /device:TPU:1, one launch (start us, length us, event | category | flops | bytes accessed | tf_op | source)
XLA Modules:
  0.0 118.4 jit_solution(12172939268634587955)
XLA Ops:
  0.0 4.1 %shard_map.82 = (bf16[1040,128]{1,0:T(8,128)(2,1)S(1)}, bf16[128,128]{1,0:T(8,128)(2,1)S(1)}, f32[128,128]{1,0:T(8,128)S(1)}) custom-call(bf16[128,32,384]{2,1,0:T(8,128)(2,1)} %bitcast.28, f32[12,1,128]{2,1,0:T(1,128)} %bitcast.31, s32[32,128]{1,0:T(8,128)} %bitcast.30, s32[1,64]{1,0:T(1,128)} %bitcast.32, s32[1,128]{1,0:T(1,128)} %bitcast.33, ...), custom_call_target="tpu_custom_call" | custom-call | flops 1000000 | bytes 1048576 | tf_op jit(solution)/shard_map/pallas_call | solution.py:245
  4.1 5.2 %collective-permute-start.2 = (bf16[1040,128]{1,0:T(8,128)(2,1)S(1)}, bf16[1040,128]{1,0:T(8,128)(2,1)S(1)}, u32[]{:S(2)}, u32[]{:S(2)}) collective-permute-start(bf16[1040,128]{1,0:T(8,128)(2,1)S(1)} %get-tuple-element.12.w0), channel_id=1, source_target_pairs={{0,384},{64,448},{128,0},{192,64},{256,128},{320,192},{384,256},{4... | collective-permute-start | bytes 798728 | tf_op jit(solution)/shard_map/ppermute | solution.py:270
  9.4 2.4 %collective-permute-start.1 = (bf16[1040,128]{1,0:T(8,128)(2,1)S(1)}, bf16[1040,128]{1,0:T(8,128)(2,1)S(1)}, u32[]{:S(2)}, u32[]{:S(2)}) collective-permute-start(bf16[1040,128]{1,0:T(8,128)(2,1)S(1)} %get-tuple-element.12.w0), channel_id=1, source_target_pairs={{0,256},{64,320},{128,384},{192,448},{256,0},{320,64},{384,128},{4... | collective-permute-start | bytes 798728 | tf_op jit(solution)/shard_map/ppermute | solution.py:270
  11.8 2.5 %collective-permute-start = (bf16[1040,128]{1,0:T(8,128)(2,1)S(1)}, bf16[1040,128]{1,0:T(8,128)(2,1)S(1)}, u32[]{:S(2)}, u32[]{:S(2)}) collective-permute-start(bf16[1040,128]{1,0:T(8,128)(2,1)S(1)} %get-tuple-element.12.w0), channel_id=1, source_target_pairs={{0,128},{64,192},{128,256},{192,320},{256,384},{320,448},{384,0},{... | collective-permute-start | bytes 798728 | tf_op jit(solution)/shard_map/ppermute | solution.py:270
  14.3 27.0 %all_to_all.30 = bf16[64,2,128]{2,1,0:T(2,128)(2,1)S(1)} all-to-all(bf16[64,2,128]{2,1,0:T(2,128)(2,1)S(1)} %bitcast.26), channel_id=1, replica_groups=mesh['pb'=8,'ka'=64] {'ka'}, dimensions={0} | all-to-all | bytes 65536 | tf_op jit(solution)/shard_map/all_to_all | solution.py:235
  41.3 0.2 shard_map.83
  41.5 12.4 %all_to_all.31.parts_ref = bf16[8,104,128]{2,1,0:T(8,128)(2,1)S(1)} all-to-all(bf16[8,104,128]{2,1,0:T(8,128)(2,1)S(1)} %shard_map.83), channel_id=1, replica_groups=mesh['pb'=8,'ka'=64] {'pb'}, dimensions={0} | all-to-all | bytes 425984 | tf_op jit(solution)/shard_map/all_to_all | solution.py:275
  53.9 0.0 collective-permute-done.2.w3
  53.9 0.0 collective-permute-done.1.w2
  53.9 0.0 collective-permute-done.w1
  53.9 0.5 shard_map.84
  54.4 14.7 %all_to_all.32 = bf16[64,2,128]{2,1,0:T(2,128)(2,1)S(1)} all-to-all(bf16[64,2,128]{2,1,0:T(2,128)(2,1)S(1)} %bitcast.27), channel_id=1, replica_groups=mesh['pb'=8,'ka'=64] {'ka'}, dimensions={0} | all-to-all | bytes 65536 | tf_op jit(solution)/shard_map/all_to_all | solution.py:235
  69.1 0.2 shard_map.85.mine_ref
  69.3 4.0 %collective-permute-start.3 = (bf16[32,128]{1,0:T(8,128)(2,1)S(1)}, bf16[32,128]{1,0:T(8,128)(2,1)S(1)}, u32[]{:S(2)}, u32[]{:S(2)}) collective-permute-start(bf16[32,128]{1,0:T(8,128)(2,1)S(1)} %shard_map.85.mine_ref), channel_id=1, source_target_pairs={{0,64},{64,0},{128,192},{192,128},{256,320},{320,256},{384,448},{4... | collective-permute-start | bytes 24584 | tf_op jit(solution)/shard_map/ppermute | solution.py:281
  73.3 0.8 collective-permute-done.3.other_ref
  74.1 0.5 shard_map.86
  74.6 14.7 %all_to_all.33 = bf16[64,2,128]{2,1,0:T(2,128)(2,1)S(1)} all-to-all(bf16[64,2,128]{2,1,0:T(2,128)(2,1)S(1)} %bitcast.21), channel_id=1, replica_groups=mesh['pb'=8,'ka'=64] {'ka'}, dimensions={0} | all-to-all | bytes 65536 | tf_op jit(solution)/shard_map/all_to_all | solution.py:235
  89.3 0.2 shard_map.87.mine_ref
  89.5 3.4 %collective-permute-start.4 = (bf16[32,128]{1,0:T(8,128)(2,1)S(1)}, bf16[32,128]{1,0:T(8,128)(2,1)S(1)}, u32[]{:S(2)}, u32[]{:S(2)}) collective-permute-start(bf16[32,128]{1,0:T(8,128)(2,1)S(1)} %shard_map.87.mine_ref), channel_id=1, source_target_pairs={{0,64},{64,0},{128,192},{192,128},{256,320},{320,256},{384,448},{4... | collective-permute-start | bytes 24584 | tf_op jit(solution)/shard_map/ppermute | solution.py:281
  92.9 0.8 collective-permute-done.4.other_ref
  93.7 0.5 shard_map.88
  94.1 14.7 %all_to_all.34 = bf16[64,2,128]{2,1,0:T(2,128)(2,1)S(1)} all-to-all(bf16[64,2,128]{2,1,0:T(2,128)(2,1)S(1)} %bitcast.20), channel_id=1, replica_groups=mesh['pb'=8,'ka'=64] {'ka'}, dimensions={0} | all-to-all | bytes 65536 | tf_op jit(solution)/shard_map/all_to_all | solution.py:235
  108.8 0.2 shard_map.89
  109.0 8.7 %all_to_all.35.parts_ref = bf16[8,32,128]{2,1,0:T(8,128)(2,1)S(1)} all-to-all(bf16[8,32,128]{2,1,0:T(8,128)(2,1)S(1)} %shard_map.89), channel_id=1, replica_groups=mesh['pb'=8,'ka'=64] {'pb'}, dimensions={0} | all-to-all | bytes 131072 | tf_op jit(solution)/shard_map/all_to_all | solution.py:287
  117.7 0.6 shard_map.90
Async XLA Ops:
  4.1 49.8 %collective-permute-start.2 = (bf16[1040,128]{1,0:T(8,128)(2,1)S(1)}, bf16[1040,128]{1,0:T(8,128)(2,1)S(1)}, u32[]{:S(2)}, u32[]{:S(2)}) collective-permute-start(bf16[1040,128]{1,0:T(8,128)(2,1)S(1)} %get-tuple-element.12.w0), channel_id=1, source_target_pairs={{0,384},{64,448},{128,0},{192,64},{256,128},{320,192},{384,256},{4... | collective-permute-start | bytes 798728 | tf_op jit(solution)/shard_map/ppermute | solution.py:270
  9.4 44.6 %collective-permute-start.1 = (bf16[1040,128]{1,0:T(8,128)(2,1)S(1)}, bf16[1040,128]{1,0:T(8,128)(2,1)S(1)}, u32[]{:S(2)}, u32[]{:S(2)}) collective-permute-start(bf16[1040,128]{1,0:T(8,128)(2,1)S(1)} %get-tuple-element.12.w0), channel_id=1, source_target_pairs={{0,256},{64,320},{128,384},{192,448},{256,0},{320,64},{384,128},{4... | collective-permute-start | bytes 798728 | tf_op jit(solution)/shard_map/ppermute | solution.py:270
  11.8 42.1 %collective-permute-start = (bf16[1040,128]{1,0:T(8,128)(2,1)S(1)}, bf16[1040,128]{1,0:T(8,128)(2,1)S(1)}, u32[]{:S(2)}, u32[]{:S(2)}) collective-permute-start(bf16[1040,128]{1,0:T(8,128)(2,1)S(1)} %get-tuple-element.12.w0), channel_id=1, source_target_pairs={{0,128},{64,192},{128,256},{192,320},{256,384},{320,448},{384,0},{... | collective-permute-start | bytes 798728 | tf_op jit(solution)/shard_map/ppermute | solution.py:270
  69.3 4.8 %collective-permute-start.3 = (bf16[32,128]{1,0:T(8,128)(2,1)S(1)}, bf16[32,128]{1,0:T(8,128)(2,1)S(1)}, u32[]{:S(2)}, u32[]{:S(2)}) collective-permute-start(bf16[32,128]{1,0:T(8,128)(2,1)S(1)} %shard_map.85.mine_ref), channel_id=1, source_target_pairs={{0,64},{64,0},{128,192},{192,128},{256,320},{320,256},{384,448},{4... | collective-permute-start | bytes 24584 | tf_op jit(solution)/shard_map/ppermute | solution.py:281
  89.5 4.2 %collective-permute-start.4 = (bf16[32,128]{1,0:T(8,128)(2,1)S(1)}, bf16[32,128]{1,0:T(8,128)(2,1)S(1)}, u32[]{:S(2)}, u32[]{:S(2)}) collective-permute-start(bf16[32,128]{1,0:T(8,128)(2,1)S(1)} %shard_map.87.mine_ref), channel_id=1, source_target_pairs={{0,64},{64,0},{128,192},{192,128},{256,320},{320,256},{384,448},{4... | collective-permute-start | bytes 24584 | tf_op jit(solution)/shard_map/ppermute | solution.py:281
